TPU v7x, 256 devices: a whole 4x4x8 slice. The times are simulated.
256 devices in a mesh: vocab: 32 (over y, z), batch: 8 (over x, core).
Axes of the slice: x: 4, y: 4, z: 8, core: 2. Of those that a mesh axis runs over, the one named last changes fastest.
Arguments:
- tokens: bfloat16 [2048, 5120], P('batch'), may hold values from -180 to 180
- cluster_ids: int32 [2048, 1], P('batch'), may hold values from 0 to 3; in each aligned block of 256 rows (0 to 255, 256 to 511, ...) at most 128 rows name the same one
- head_weight: bfloat16 [5120, 16384], P('batch', 'vocab'), may hold values from -0.078125 to 0.078125
- cluster_weight: bfloat16 [5120, 4], replicated, may hold values from -0.078125 to 0.078125
- tail_proj: bfloat16 [5120, 2400], P('vocab'), may hold values from -0.078125 to 0.078125
- out_one: bfloat16 [1280, 16384], P(None, 'vocab'), may hold values from -0.15625 to 0.15625
- out_two: bfloat16 [640, 32768], P(None, 'vocab'), may hold values from -0.25 to 0.25
- out_three: bfloat16 [320, 32768], P(None, 'vocab'), may hold values from -0.3125 to 0.3125
- out_four: bfloat16 [160, 32768], P(None, 'vocab'), may hold values from -0.5 to 0.5
Outputs:
- head_logp: float32 [2048, 16384], P('batch', 'vocab')
- tail_one: float32 [1024, 16384], P('batch', 'vocab')
- tail_two: float32 [1024, 32768], P('batch', 'vocab')
- tail_three: float32 [1024, 32768], P('batch', 'vocab')
- tail_four: float32 [1024, 32768], P('batch', 'vocab')
Inputs may be any that keep to these rules, and one draw needn't show every extreme that they name: `cluster_ids`: in the 256 rows of one index of batch no cluster is named by more than 128 rows.
All inputs are finite; a program needn't handle non-finite values.
Results may differ from a plain program's by a relative error of at most 0.00057.
Values may be sent and summed in bfloat16 or wider, within the bound.
A program may use at most 64 MiB of HBM per device.

v0:
```python
import jax
import jax.numpy as jnp
from jax import lax
from jax.sharding import PartitionSpec as P

CLUSTERS = 4
CAP = 128


def sent_to_all(array, axis):
    copies = jnp.broadcast_to(array, (lax.axis_size(axis), *array.shape))
    return lax.all_to_all(copies, axis, split_axis=0, concat_axis=0, tiled=True)


def all_in_one(array, axis):
    leaves = jax.tree.leaves(array)
    sequence = sorted(range(len(leaves)), key=lambda k: -leaves[k].size)
    width = (1, *leaves[sequence[0]].shape)[-1]
    lines = [
        jnp.pad(leaves[k].reshape(-1), (0, -leaves[k].size % width)).reshape(-1, width)
        for k in sequence
    ]
    both, at, found = (sent_to_all(jnp.concatenate(lines), axis), 0, {})
    for k, line in zip(sequence, lines):
        share = both[:, at : at + len(line)].reshape(len(both), -1)
        found[k] = share[:, : leaves[k].size].reshape(-1, *leaves[k].shape)
        at += len(line)
    numbers = iter(range(len(leaves)))
    return jax.tree.map(lambda _: found[next(numbers)], array)


def combined_pairwise(pieces, combine):
    while len(jax.tree.leaves(pieces)[0]) > 1:
        pieces = jax.vmap(combine)(
            *(jax.tree.map(lambda part: part[side::2], pieces) for side in (0, 1))
        )
    return jax.tree.map(lambda part: part[0], pieces)


def merged(array, axis, combine):
    pieces = all_in_one(array, axis)
    return combined_pairwise(pieces, combine)


def in_blocks(array, dim, peers):
    lengths = array.shape
    tiles = array.reshape(*lengths[:dim], peers, lengths[dim] // peers, *lengths[dim + 1 :])
    return jnp.moveaxis(tiles, dim, 0)


def summed_on_arrival(array, axis, dim):
    tiles = in_blocks(array, dim, lax.axis_size(axis))
    arrived = lax.all_to_all(tiles, axis, split_axis=0, concat_axis=0, tiled=True)
    return arrived.sum(axis=0)


def laid_out(tiles, dim):
    tiles = jnp.moveaxis(tiles, 0, dim)
    lengths = tiles.shape
    return tiles.reshape(*lengths[:dim], lengths[dim] * lengths[dim + 1], *lengths[dim + 2 :])


def collect(array, axis, dim):
    return laid_out(sent_to_all(array, axis), dim)


def merge_pair(earlier, later_one):
    highest = jnp.maximum(earlier[0], later_one[0])
    return (
        highest,
        earlier[1] * jnp.exp(earlier[0] - highest) + later_one[1] * jnp.exp(later_one[0] - highest),
    )


def local_totals(logits):
    highest = jnp.max(logits, axis=-1)
    return (highest, jnp.sum(jnp.exp(logits - highest[:, None]), axis=-1))


def shards(
    tokens,
    cluster_ids,
    head_weight,
    cluster_weight,
    tail_proj,
    out_one,
    out_two,
    out_three,
    out_four,
):
    head_logits = jnp.dot(
        tokens,
        lax.all_gather(head_weight, "batch", axis=0, tiled=True),
        preferred_element_type=jnp.float32,
    )
    cluster_logits = jnp.dot(tokens, cluster_weight, preferred_element_type=jnp.float32)
    head_top, head_sum = merged(local_totals(head_logits), "vocab", merge_pair)
    overall = jnp.maximum(head_top, jnp.max(cluster_logits, axis=1))
    denominator = head_sum * jnp.exp(head_top - overall) + jnp.sum(
        jnp.exp(cluster_logits - overall[:, None]), axis=1
    )
    log_total = overall + jnp.log(denominator)
    head_logp = head_logits - log_total[:, None]
    cluster_logp = cluster_logits - log_total[:, None]
    feature_count = tail_proj.shape[0]
    own_cols = lax.dynamic_slice_in_dim(
        tokens, lax.axis_index("vocab") * feature_count, feature_count, 1
    )
    cluster_of = cluster_ids[:, 0]
    labels = jnp.arange(CLUSTERS, dtype=jnp.int32)
    onehot = (cluster_of[:, None] == labels[None, :]).astype(jnp.int32)
    before = jnp.cumsum(onehot, axis=0) - onehot
    slot_of = jnp.sum(before * onehot, axis=1)
    slot_numbers = jnp.arange(CAP, dtype=jnp.int32)
    picker = (
        (cluster_of[None, None, :] == labels[:, None, None])
        & (slot_of[None, None, :] == slot_numbers[None, :, None])
    ).astype(jnp.bfloat16)
    blocks = jnp.einsum("cjs,sd->cjd", picker, own_cols, preferred_element_type=jnp.float32).astype(
        jnp.bfloat16
    )
    picker_wide = picker.astype(jnp.float32)
    slot_logp = jnp.einsum("cjs,sc->cj", picker_wide, cluster_logp, precision=lax.Precision.HIGHEST)
    occupied = jnp.sum(picker_wide, axis=2) > 0
    out_weights = (out_one, out_two, out_three, out_four)
    widths = [weight.shape[0] for weight in out_weights]
    partials = []
    offset = 0
    for cluster in range(CLUSTERS):
        partials.append(
            jnp.dot(
                blocks[cluster],
                tail_proj[:, offset : offset + widths[cluster]],
                preferred_element_type=jnp.float32,
            )
        )
        offset = offset + widths[cluster]
    partial_value = jnp.concatenate(partials, axis=1)
    shares = summed_on_arrival(partial_value, "vocab", 1).astype(jnp.bfloat16)
    projected = collect(shares, "vocab", 1)
    scores = []
    offset = 0
    for cluster in range(CLUSTERS):
        scores.append(
            jnp.dot(
                projected[:, offset : offset + widths[cluster]],
                out_weights[cluster],
                preferred_element_type=jnp.float32,
            )
        )
        offset = offset + widths[cluster]
    block_top = jnp.stack([jnp.max(each_score, axis=1) for each_score in scores], axis=1)
    block_sum = jnp.stack(
        [
            jnp.sum(jnp.exp(scores[cluster] - block_top[:, cluster][:, None]), axis=1)
            for cluster in range(CLUSTERS)
        ],
        axis=1,
    )
    tail_top, tail_sum = merged((block_top, block_sum), "vocab", merge_pair)
    tail_log = tail_top + jnp.log(tail_sum)
    results = []
    for cluster in range(CLUSTERS):
        shifted = scores[cluster] - (tail_log[:, cluster] - slot_logp[cluster])[:, None]
        results.append(jnp.where(occupied[cluster][:, None], shifted, jnp.zeros_like(shifted)))
    return (head_logp, results[0], results[1], results[2], results[3])


def solution(mesh):
    in_specs = (
        P("batch", None),
        P("batch", None),
        P("batch", "vocab"),
        P(),
        P("vocab", None),
        P(None, "vocab"),
        P(None, "vocab"),
        P(None, "vocab"),
        P(None, "vocab"),
    )
    out_specs = (
        P("batch", "vocab"),
        P("batch", "vocab"),
        P("batch", "vocab"),
        P("batch", "vocab"),
        P("batch", "vocab"),
    )
    return jax.shard_map(shards, mesh=mesh, in_specs=in_specs, out_specs=out_specs, check_vma=False)
```

profile of v0, /device:TPU:6, one launch (start us, length us, event | category | flops | bytes accessed | tf_op | source)
XLA Modules:
  0.0 160.6 jit_solution(950733718774872792)
XLA Ops:
  7.2 0.0 copy-start
  7.2 0.0 all-gather.2.cloned.1.call-start
  7.2 0.7 all-gather.2.cloned.1.call-update
  7.9 0.7 compare_convert_fusion
  8.6 1.2 reduce-window.6
  9.8 0.1 slice.294
  9.9 0.1 copy.21
  10.1 0.1 copy.22
  10.2 0.1 add_bitcast_fusion
  10.2 0.7 fusion.27
  10.9 0.7 iota_compare_fusion.2
  11.7 0.0 copy-done
  11.7 0.0 copy-start.7
  11.7 0.3 convolution_convert_fusion
  12.0 1.8 %fusion.21 = f32[128,160]{1,0:T(8,128)} fusion(bf16[160,2400]{1,0:T(8,128)(2,1)} %param.13, bf16[4,128,160]{1,2,0:T(8,128)(2,1)S(1)} %convolution_convert_fusion), kind=kOutput, calls=%fused_computation.35 | convolution fusion | flops 6553600 | bytes 204800 | tf_op jit(solution)/shard_map/dot_general | solution.py:131
  13.8 1.1 fusion.17
  14.9 1.9 %fusion.11 = f32[128,640]{1,0:T(8,128)} fusion(bf16[160,2400]{1,0:T(8,128)(2,1)} %param.13, bf16[4,128,160]{1,2,0:T(8,128)(2,1)S(1)} %convolution_convert_fusion), kind=kOutput, calls=%fused_computation.24 | convolution fusion | flops 26214400 | bytes 573440 | tf_op jit(solution)/shard_map/dot_general | solution.py:131
  16.8 1.3 fusion.3
  18.1 2.1 %concatenate.10 = f32[128,2400]{1,0:T(8,128)} concatenate(f32[128,1280]{1,0:T(8,128)S(1)} %fusion.3, f32[128,640]{1,0:T(8,128)} %fusion.11, f32[128,320]{1,0:T(8,128)S(1)} %fusion.17, f32[128,160]{1,0:T(8,128)} %fusion.21), dimensions={1} | concatenate | bytes 2457600 | tf_op jit(solution)/shard_map/concatenate | solution.py:138
  20.2 2.7 %copy.26 = f32[128,2400]{0,1:T(8,128)} copy(f32[128,2400]{1,0:T(8,128)} %concatenate.10) | data formatting | bytes 2457600 | tf_op jit(solution)/shard_map/concatenate | solution.py:138
  22.9 2.5 %reshape.144 = f32[128,32,75]{0,2,1:T(8,128)} reshape(f32[128,2400]{0,1:T(8,128)} %copy.26) | data formatting | bytes 2457600 | tf_op jit(solution)/shard_map/reshape | solution.py:47
  25.4 46.7 %all_to_all.20 = f32[32,128,75]{1,2,0:T(8,128)} all-to-all(f32[32,128,75]{1,2,0:T(8,128)} %bitcast.105), channel_id=1, replica_groups=mesh['vocab'=32,'batch'=8] {'vocab'}, dimensions={0} | all-to-all | bytes 2457600 | tf_op jit(solution)/shard_map/all_to_all | solution.py:53
  72.1 1.4 reduce_sum.85
  73.5 0.9 broadcast_in_dim.61
  74.5 4.4 %all-to-all-start.2 = ((bf16[32,128,75]{1,2,0:T(8,128)(2,1)}), bf16[32,128,75]{1,2,0:T(8,128)(2,1)S(1)}, u32[]{:S(2)}, u32[]{:S(2)}) async-start(bf16[32,128,75]{1,2,0:T(8,128)(2,1)} %broadcast_in_dim.61), calls=%async_computation.2 | async-start | bytes 1310720 | tf_op jit(solution)/shard_map/all_to_all | solution.py:12
  78.8 0.0 copy-done.7
  78.9 0.2 convert_reduce_fusion
  79.0 0.0 copy-done.9
  79.0 0.8 fusion.43
  79.8 19.4 %all-to-all-done.2 = bf16[32,128,75]{1,2,0:T(8,128)(2,1)S(1)} async-done(((bf16[32,128,75]{1,2,0:T(8,128)(2,1)}), bf16[32,128,75]{1,2,0:T(8,128)(2,1)S(1)}, u32[]{:S(2)}, u32[]{:S(2)}) %all-to-all-start.2) | async-done | bytes 614432 | tf_op jit(solution)/shard_map/all_to_all | solution.py:12
  99.2 1.0 reshape.145
  100.2 2.0 %fusion.47 = (f32[128]{0:T(128)S(1)}, f32[128,512]{1,0:T(8,128)S(1)}) fusion(bf16[1280,512]{1,0:T(8,128)(2,1)} %param.14, bf16[128,2400]{0,1:T(8,128)(2,1)} %reshape.145), kind=kOutput, calls=%fused_computation.104 | convolution fusion | flops 167837568 | bytes 1901056 | tf_op jit(solution)/shard_map/dot_general | solution.py:145
  102.2 0.2 exponential_reduce_fusion.4
  102.4 1.3 fusion.44
  103.8 0.2 exponential_reduce_fusion
  104.0 0.0 copy-done.6
  104.0 1.3 fusion.45
  105.3 0.8 copy-done.1
  106.1 0.2 exponential_reduce_fusion.1
  106.3 1.4 fusion.46
  107.7 0.0 copy-start.3
  107.7 0.8 copy-done.3
  108.5 0.2 exponential_reduce_fusion.2
  108.8 0.7 broadcast_in_dim.62
  109.4 4.8 %all-to-all-start.3 = ((f32[32,256,4]{1,2,0:T(4,128)}), f32[32,256,4]{1,2,0:T(4,128)S(1)}, u32[]{:S(2)}, u32[]{:S(2)}) async-start(f32[32,256,4]{1,2,0:T(4,128)} %broadcast_in_dim.62), calls=%async_computation.3 | async-start | bytes 262144 | tf_op jit(solution)/shard_map/all_to_all | solution.py:12
  114.2 0.6 slice_bitcast_fusion.8
  114.8 9.8 %all-to-all-done.3 = f32[32,256,4]{1,2,0:T(4,128)S(1)} async-done(((f32[32,256,4]{1,2,0:T(4,128)}), f32[32,256,4]{1,2,0:T(4,128)S(1)}, u32[]{:S(2)}, u32[]{:S(2)}) %all-to-all-start.3) | async-done | bytes 131104 | tf_op jit(solution)/shard_map/all_to_all | solution.py:12
  124.8 0.0 copy-start.8
  124.8 0.0 all-gather.2.cloned.1.call-done
  124.8 4.1 %fusion.42 = (f32[256]{0:T(256)S(1)}, f32[256,512]{1,0:T(8,128)S(1)}) fusion(bf16[256,5120]{1,0:T(8,128)(2,1)S(1)} %copy-done, bf16[5120,512]{1,0:T(8,128)(2,1)} %all-gather.2.cloned.1.call-done), kind=kOutput, calls=%fused_computation.99 | convolution fusion | flops 1342308096 | bytes 8389632 | tf_op jit(solution)/shard_map/dot_general | solution.py:91
  128.9 0.0 copy-start.4
  128.9 0.8 copy-done.4
  129.7 0.2 exponential_reduce_fusion.3
  129.9 0.7 broadcast_in_dim.58
  130.6 3.9 %all-to-all-start = ((f32[32,2,256]{2,1,0:T(2,128)}), f32[32,2,256]{2,1,0:T(2,128)S(1)}, u32[]{:S(2)}, u32[]{:S(2)}) async-start(f32[32,2,256]{2,1,0:T(2,128)} %broadcast_in_dim.58), calls=%async_computation | async-start | bytes 131072 | tf_op jit(solution)/shard_map/all_to_all | solution.py:12
  134.4 10.0 %all-to-all-done = f32[32,2,256]{2,1,0:T(2,128)S(1)} async-done(((f32[32,2,256]{2,1,0:T(2,128)}), f32[32,2,256]{2,1,0:T(2,128)S(1)}, u32[]{:S(2)}, u32[]{:S(2)}) %all-to-all-start) | async-done | bytes 65568 | tf_op jit(solution)/shard_map/all_to_all | solution.py:12
  144.4 0.1 fusion.41
  145.0 2.0 %broadcast_subtract_fusion = f32[256,512]{1,0:T(8,128)} fusion(f32[256,512]{1,0:T(8,128)} %copy-done.4, f32[256]{0:T(256)S(1)} %log_add_fusion), kind=kLoop, calls=%fused_computation.19 | loop fusion | flops 131072 | bytes 1049600 | tf_op jit(solution)/shard_map/sub | solution.py:103
  147.0 0.0 copy-done.8
  147.0 0.3 fusion
  147.3 1.4 subtract_select_fusion.3
  148.7 2.0 %subtract_select_fusion.2 = f32[128,1024]{1,0:T(8,128)} fusion(f32[128,1024]{1,0:T(8,128)} %copy-done.3, f32[128]{0:T(128)S(1)} %get-tuple-element.29, pred[128]{0:T(512)(128)(4,1)} %get-tuple-element.33), kind=kLoop, calls=%fused_computation.7 | loop fusion | flops 262144 | bytes 1049216 | tf_op jit(solution)/shard_map/jit(_where)/select_n | solution.py:165
  150.7 1.6 subtract_select_fusion.1
  152.3 1.5 subtract_select_fusion
  (46 shorter events, 0.7 us)
Async XLA Ops:
  7.2 4.5 %copy-start = (bf16[256,5120]{1,0:T(8,128)(2,1)S(1)}, bf16[256,5120]{1,0:T(8,128)(2,1)}, u32[]{:S(2)}) copy-start(bf16[256,5120]{1,0:T(8,128)(2,1)} %param.9) | copy-start | bytes 7864324
  7.2 117.6 %all-gather.2.cloned.1.call-start = ((), (), s32[]{:S(2)}) async-start(), calls=%async_computation.4 | async-start | bytes 5898240 | tf_op jit(solution)/shard_map/all_gather | solution.py:93
  11.7 67.2 %copy-start.7 = (pred[128,256]{1,0:T(8,128)(4,1)}, pred[128,256]{1,0:T(8,128)(4,1)S(1)}, u32[]{:S(2)}) copy-start(pred[128,256]{1,0:T(8,128)(4,1)S(1)} %iota_compare_fusion) | copy-start | bytes 98308
  25.4 53.6 %copy-start.9 = (bf16[5120,4]{0,1:T(4,128)(2,1)S(1)}, bf16[5120,4]{0,1:T(4,128)(2,1)}, u32[]{:S(2)}) copy-start(bf16[5120,4]{0,1:T(4,128)(2,1)} %param.12) | copy-start | bytes 122884
  74.5 24.7 %all-to-all-start.2 = ((bf16[32,128,75]{1,2,0:T(8,128)(2,1)}), bf16[32,128,75]{1,2,0:T(8,128)(2,1)S(1)}, u32[]{:S(2)}, u32[]{:S(2)}) async-start(bf16[32,128,75]{1,2,0:T(8,128)(2,1)} %broadcast_in_dim.61), calls=%async_computation.2 | async-start | bytes 1310720 | tf_op jit(solution)/shard_map/all_to_all | solution.py:12
  100.2 3.8 %copy-start.6 = (bf16[320,1024]{1,0:T(8,128)(2,1)S(1)}, bf16[320,1024]{1,0:T(8,128)(2,1)}, u32[]{:S(2)}) copy-start(bf16[320,1024]{1,0:T(8,128)(2,1)} %param.16) | copy-start | bytes 1966084
  100.2 6.1 %copy-start.5 = (bf16[640,1024]{1,0:T(8,128)(2,1)S(1)}, bf16[640,1024]{1,0:T(8,128)(2,1)}, u32[]{:S(2)}) copy-start(bf16[640,1024]{1,0:T(8,128)(2,1)} %param.15) | copy-start | bytes 3932164
  105.3 0.8 copy-start.1
  107.7 0.8 copy-start.3
  109.4 15.2 %all-to-all-start.3 = ((f32[32,256,4]{1,2,0:T(4,128)}), f32[32,256,4]{1,2,0:T(4,128)S(1)}, u32[]{:S(2)}, u32[]{:S(2)}) async-start(f32[32,256,4]{1,2,0:T(4,128)} %broadcast_in_dim.62), calls=%async_computation.3 | async-start | bytes 262144 | tf_op jit(solution)/shard_map/all_to_all | solution.py:12
  124.8 22.2 %copy-start.8 = (pred[128,256]{1,0:T(8,128)(4,1)S(1)}, pred[128,256]{1,0:T(8,128)(4,1)}, u32[]{:S(2)}) copy-start(pred[128,256]{1,0:T(8,128)(4,1)} %copy-done.7) | copy-start | bytes 98308
  128.9 0.8 copy-start.4
  130.6 13.9 %all-to-all-start = ((f32[32,2,256]{2,1,0:T(2,128)}), f32[32,2,256]{2,1,0:T(2,128)S(1)}, u32[]{:S(2)}, u32[]{:S(2)}) async-start(f32[32,2,256]{2,1,0:T(2,128)} %broadcast_in_dim.58), calls=%async_computation | async-start | bytes 131072 | tf_op jit(solution)/shard_map/all_to_all | solution.py:12
  144.9 5.8 %copy-start.2 = (f32[128,1024]{1,0:T(8,128)S(1)}, f32[128,1024]{1,0:T(8,128)}, u32[]{:S(2)}) copy-start(f32[128,1024]{1,0:T(8,128)} %copy-done.1) | copy-start | bytes 1572868
Sparse Core Ops, SparseCore 0:
  9.8 40.0 all-gather.1
where the time goes:
time: 162 us; the launch traced here: 161 us
  blocking collectives  46.7 us (29%)
  waiting for transfers between devices  39.8 us (25%)
  matrix products  17.6 us (11%)
  other arithmetic  14.8 us (9%)
  local copies, waits for them, and re-layouts  14.3 us (9%)
  between operations  14.3 us (9%)
  starting transfers between devices  13 us (8%)
    all_to_all x1, blocking collectives, summed_on_arrival(): lax.all_to_all(tiles, axis, split_axis=0, concat_axis=0, tiled=True)  46.7 us
    all_to_all x3, waiting for transfers between devices, sent_to_all(): return lax.all_to_all(copies, axis, split_axis=0, concat_axis=0, tiled=True)  39.1 us
    all_to_all x3, starting transfers between devices, sent_to_all(): return lax.all_to_all(copies, axis, split_axis=0, concat_axis=0, tiled=True)  13 us
    select_n x4, other arithmetic, shards(): jnp.where(occupied[cluster][:, None], shifted, jnp.zeros_like(shifted))  6.48 us
    dot_general x4, matrix products, shards(): jnp.dot(blocks[cluster], tail_proj[:, offset:offset + widths[cluster]], p...  6.05 us
    dot_general x4, matrix products, shards(): jnp.dot(projected[:, offset:offset + widths[cluster]], out_weights[cluste...  6.02 us
    concatenate x2, local copies, waits for them, and re-layouts, shards(): partial_value = jnp.concatenate(partials, axis=1)  4.81 us
    dot_general x1, matrix products, shards(): jnp.dot(tokens, lax.all_gather(head_weight, 'batch', axis=0, tiled=True),...  4.08 us
  transfers between devices with their start and end apart: 4, of which 3 were waited for; matrix products, arithmetic and copies ran while one was open for 19% of the time, Pallas kernels for 0%

commit v1 on v0

v1 whole, which is shorter than its diff:
```python
import jax
import jax.numpy as jnp
from jax import lax
from jax.experimental import pallas as pl
from jax.experimental.pallas import tpu as pltpu
from jax.sharding import PartitionSpec as P

NY, NZ, NX = 4, 8, 4
NV = NY * NZ
NB = 2 * NX
TILES = 19
F32, BF16 = jnp.float32, jnp.bfloat16


def ring_place(i, y):
    return lax.rem((i * 8) // 5 + 2 * y, NZ)


def remote(src, dst, send_sem, recv_sem, v, b):
    return pltpu.make_async_remote_copy(
        src_ref=src,
        dst_ref=dst,
        send_sem=send_sem,
        recv_sem=recv_sem,
        device_id=(v, b),
        device_id_type=pl.DeviceIdType.MESH,
    )


def arrived(ref, sem):
    pltpu.make_async_copy(ref, ref, sem).wait()


def log_sum(x):
    top = jnp.max(x, axis=1, keepdims=True)
    return top + jnp.log(jnp.sum(jnp.exp(x - top), axis=1, keepdims=True))


def work(
    tok_h, ids_h, w_h, cw_h, t_h, o1_h, o2_h, o3_h, o4_h,
    head_o, s1_o, s2_o, s3_o, s4_o, off_o,
    tok, ids, wbuf, cw, tin, tv, town, pbuf, o1, o2, o3, o4, msg, xbuf, pick, rows,
    ld_w, ld_tok, ld_misc,
    wss, wrs, tss, trs, tpss, tprs, pzss, pzrs, pyss, pyrs, poss, pors, xss, xrs,
):
    v, b = lax.axis_index("vocab"), lax.axis_index("batch")
    y, z = v // NZ, lax.rem(v, NZ)
    x, c = b // 2, lax.rem(b, 2)
    right = lax.rem(x + 1, NX) * 2 + c
    left = lax.rem(x + 3, NX) * 2 + c
    far = lax.rem(x + 2, NX) * 2 + c
    mate = x * 2 + 1 - c
    y_up, y_down, y_far = lax.rem(y + 1, NY), lax.rem(y + 3, NY), lax.rem(y + 2, NY)

    load_t = pltpu.make_async_copy(t_h, tin, ld_misc.at[0])
    load_t.start()
    load_w = [
        pltpu.make_async_copy(w_h.at[:, pl.ds(128 * q, 128)], wbuf.at[b, q], ld_w.at[q])
        for q in range(4)
    ]
    for copy in load_w:
        copy.start()
    load_ids = pltpu.make_async_copy(ids_h, ids, ld_misc.at[1])
    load_ids.start()
    load_cw = pltpu.make_async_copy(cw_h, cw, ld_misc.at[2])
    load_cw.start()
    load_tok = [
        pltpu.make_async_copy(tok_h.at[:, pl.ds(640 * k, 640)], tok.at[k], ld_tok.at[k])
        for k in range(8)
    ]
    for copy in load_tok:
        copy.start()
    load_out = [
        pltpu.make_async_copy(src, dst, ld_misc.at[3 + k])
        for k, (src, dst) in enumerate(((o1_h, o1), (o2_h, o2), (o3_h, o3), (o4_h, o4)))
    ]
    for copy in load_out:
        copy.start()

    barrier = pltpu.get_barrier_semaphore()
    for peer in (right, left, mate):
        pl.semaphore_signal(barrier, inc=1, device_id=(v, peer), device_id_type=pl.DeviceIdType.MESH)

    @pl.loop(1, NV)
    def _(k):
        pl.semaphore_signal(
            barrier, inc=1, device_id=(lax.rem(v + k, NV), b), device_id_type=pl.DeviceIdType.MESH
        )

    load_t.wait()
    for j in range(TILES - 1):
        for h in range(2):
            tv[j, h] = tin[80 * h : 80 * h + 80, 128 * j : 128 * j + 128]
    for h in range(2):
        tv[TILES - 1, h] = jnp.concatenate(
            [tin[80 * h : 80 * h + 80, 2304:2400], jnp.zeros((80, 32), BF16)], axis=1
        )
    for copy in load_w:
        copy.wait()
    pl.semaphore_wait(barrier, 3 + NV - 1)

    def w_send(shard, q, to, k):
        return remote(wbuf.at[shard, q], wbuf.at[shard, q], wss.at[k], wrs.at[shard, q], v, to)

    pending = []

    def start(copy):
        copy.start()
        pending.append(copy)

    for k in range(4):
        start(w_send(b, k, right, k))
        start(w_send(b, (k + 2) % 4, left, 4 + k))
    for k in range(4):
        start(w_send(b, k, mate, 8 + k))

    def t_send(j):
        y_to = j // 5
        v_to = y_to * NZ + ring_place(lax.rem(j, 5), y_to)
        return v_to, remote(tv.at[j, c], town.at[v, c], tss.at[j], trs.at[v], v_to, b)

    @pl.loop(0, TILES)
    def _(jj):
        v_to, copy = t_send(lax.rem(jj + v, TILES))

        @pl.when(v_to != v)
        def _():
            copy.start()

    mine_r = lax.rem(z - 2 * y + 8, NZ)
    mine_i = (5 * mine_r + 7) // 8
    mine_j = 5 * y + mine_i
    owner = jnp.logical_and((mine_i * 8) // 5 == mine_r, mine_j < TILES)

    load_ids.wait()
    id_row = ids[...]
    kinds = lax.broadcasted_iota(jnp.int32, (8, 256), 0)
    onehot = jnp.where(kinds == id_row, 1.0, 0.0).astype(F32)
    earlier = lax.broadcasted_iota(jnp.int32, (256, 256), 0) < lax.broadcasted_iota(
        jnp.int32, (256, 256), 1
    )
    before = jnp.dot(
        onehot.astype(BF16), jnp.where(earlier, 1.0, 0.0).astype(BF16), preferred_element_type=F32
    )
    slot_row = jnp.sum(onehot * before, axis=0, keepdims=True)
    slots = lax.broadcasted_iota(jnp.int32, (128, 256), 0).astype(F32)

    def mask_of(k):
        return jnp.logical_and(id_row == k, slot_row == slots)

    for k in range(4):
        pick[k] = jnp.where(mask_of(k), 1.0, 0.0).astype(BF16)
    for copy in load_tok:
        copy.wait()
    load_cw.wait()
    small = jnp.zeros((4, 256), F32)
    for k in range(8):
        small += lax.dot_general(
            cw[:, 640 * k : 640 * k + 640],
            tok[k],
            (((1,), (1,)), ((), ())),
            preferred_element_type=F32,
        )
    rows[0:4] = small
    for copy in load_out:
        copy.wait()

    def head_add(shard, q):
        cols = slice(128 * q, 128 * q + 128)
        head_o[:, cols] += jnp.dot(tok[shard], wbuf[shard, q], preferred_element_type=F32)

    for q in range(4):
        head_o[:, 128 * q : 128 * q + 128] = jnp.dot(
            tok[b], wbuf[b, q], preferred_element_type=F32
        )

    from_left = [(left, 0), (left, 1), (left, 2), (left, 3), (far, 0), (far, 1)]
    from_right = [(right, 2), (right, 3), (right, 0), (right, 1), (far, 2), (far, 3)]
    flip = 1 - 2 * c

    def w_step(s):
        for side, (shard, q) in enumerate((from_left[s], from_right[s])):
            arrived(wbuf.at[shard, q], wrs.at[shard, q])
            if s < 2:
                start(w_send(shard, q, (right, left)[side], 12 + 2 * s + side))
            start(w_send(shard, q, mate, 16 + 2 * s + side))
        for shard, q in (from_left[s], from_right[s]):
            head_add(shard, q)

    def w_mate(s):
        for shard, q in (from_left[s], from_right[s]):
            arrived(wbuf.at[shard + flip, q], wrs.at[shard + flip, q])
            head_add(shard + flip, q)

    for q in range(4):
        arrived(wbuf.at[mate, q], wrs.at[mate, q])
        head_add(mate, q)
    w_step(0)
    w_step(1)
    w_mate(0)

    z_sends = [
        remote(
            pbuf.at[mine_j],
            pbuf.at[mine_j],
            pzss.at[k - 1],
            pzrs.at[mine_j],
            y * NZ + lax.rem(z + k, NZ),
            b,
        )
        for k in range(1, NZ)
    ]

    def group_send(k):
        g = lax.rem(y + k, NY)
        part = town.at[pl.ds(8 * g, 8), c]
        return remote(part, part, tpss.at[g], tprs.at[g], v, mate)

    @pl.when(owner)
    def _():
        town[v, c] = tv[mine_j, c]
        for k in range(NY):
            g = lax.rem(y + k, NY)

            @pl.loop(0, NZ)
            def _(s):
                @pl.when(8 * g + s != v)
                def _():
                    arrived(town.at[8 * g + s, c], trs.at[8 * g + s])

            group_send(k).start()
        total = jnp.zeros((256, 128), F32)
        for k in range(NY):
            g = lax.rem(y + k, NY)
            part = town.at[pl.ds(8 * g, 8), 1 - c]
            arrived(part, tprs.at[g])
            for h in range(2):
                total += jnp.dot(
                    tok[2 * g + h],
                    town[pl.ds(8 * g + 4 * h, 4)].reshape(640, 128),
                    preferred_element_type=F32,
                )
        rounded = total.astype(BF16)
        low = (
            jnp.where(mine_j >= 10, 1, 0)
            + jnp.where(mine_j >= 15, 1, 0)
            + jnp.where(mine_j >= 18, 1, 0)
        )
        high = (
            jnp.where(mine_j >= 10, 1, 0)
            + jnp.where(mine_j >= 15, 1, 0)
            + jnp.where(mine_j >= 17, 1, 0)
        )
        lane = lax.broadcasted_iota(jnp.int32, (128, 128), 1)
        pbuf[mine_j] = jnp.where(
            lane < 64,
            jnp.dot(pick[low], rounded, preferred_element_type=F32),
            jnp.dot(pick[high], rounded, preferred_element_type=F32),
        ).astype(BF16)
        for copy in z_sends:
            copy.start()

    w_step(2)
    w_mate(1)

    def y_send(j, i, side):
        return remote(
            pbuf.at[j],
            pbuf.at[j],
            pyss.at[i, side],
            pyrs.at[j],
            (y_up, y_down)[side] * NZ + z,
            b,
        )

    def o_send(j, i, side):
        part = pbuf.at[j, pl.ds(64 * side, 64)]
        return remote(part, part, poss.at[i, side], pors.at[j, side], (y_up, y_down)[side] * NZ + z, b)

    for k in range(5):
        i = lax.rem(mine_i + k, 5)
        j = 5 * y + i

        @pl.when(j < TILES)
        def _():
            if k == 0:

                @pl.when(jnp.logical_not(owner))
                def _():
                    arrived(pbuf.at[j], pzrs.at[j])
            else:
                arrived(pbuf.at[j], pzrs.at[j])
            for side in range(2):
                y_send(j, i, side).start()

    w_step(3)
    w_mate(2)
    for i in range(5):
        for side, ring in enumerate((y_down, y_up)):
            j = 5 * ring + i

            @pl.when(j < TILES)
            def _():
                arrived(pbuf.at[j], pyrs.at[j])
                o_send(j, i, side).start()

    w_step(4)
    w_mate(3)
    for i in range(5):
        j = 5 * y_far + i

        @pl.when(j < TILES)
        def _():
            for side in range(2):
                part = pbuf.at[j, pl.ds(64 * side, 64)]
                arrived(part, pors.at[j, side])

    s1_o[...] = jnp.dot(
        jnp.concatenate([pbuf[t] for t in range(10)], axis=1), o1[...], preferred_element_type=F32
    )
    s2_o[...] = jnp.dot(
        jnp.concatenate([pbuf[t] for t in range(10, 15)], axis=1),
        o2[...],
        preferred_element_type=F32,
    )
    split = pbuf[17]
    s3_o[...] = jnp.dot(
        jnp.concatenate([pbuf[15], pbuf[16], split[:, :64]], axis=1),
        o3[...],
        preferred_element_type=F32,
    )
    s4_o[...] = jnp.dot(
        jnp.concatenate([split[:, 64:], pbuf[18][:, :96]], axis=1),
        o4[...],
        preferred_element_type=F32,
    )
    eye = lax.broadcasted_iota(jnp.int32, (128, 128), 0) == lax.broadcasted_iota(
        jnp.int32, (128, 128), 1
    )

    def as_row(col):
        return jnp.sum(jnp.where(eye, col, 0.0), axis=0, keepdims=True)

    def as_col(row):
        return jnp.sum(jnp.where(eye, row, 0.0), axis=1, keepdims=True)

    tail_rows = [as_row(log_sum(ref[...])) for ref in (s1_o, s2_o, s3_o, s4_o)]
    w_step(5)
    w_mate(4)
    w_mate(5)
    head_rows = [as_row(log_sum(head_o[128 * k : 128 * k + 128])) for k in range(2)]
    packed = jnp.concatenate(head_rows + tail_rows + [jnp.zeros((2, 128), F32)], axis=0)
    msg[...] = packed
    xbuf[v] = packed

    def x_send(k):
        to = lax.rem(v + k, NV)
        return remote(msg, xbuf.at[v], xss.at[k], xrs.at[v], to, b)

    @pl.loop(1, NV)
    def _(k):
        x_send(k).start()

    small = rows[0:4]
    small_top = jnp.max(small, axis=0, keepdims=True)
    small_sum = jnp.sum(jnp.exp(small - small_top), axis=0, keepdims=True)

    @pl.loop(1, NV)
    def _(k):
        s = lax.rem(v + k, NV)
        arrived(xbuf.at[s], xrs.at[s])

    every = xbuf[...]
    top = jnp.max(every, axis=0)
    lse = top + jnp.log(jnp.sum(jnp.exp(every - top[None]), axis=0))
    head_lse = jnp.concatenate([lse[0:1], lse[1:2]], axis=1)
    overall = jnp.maximum(head_lse, small_top)
    total_row = overall + jnp.log(
        jnp.exp(head_lse - overall) + small_sum * jnp.exp(small_top - overall)
    )
    lane = lax.broadcasted_iota(jnp.int32, (128, 128), 1)
    found = jnp.zeros((128, 128), F32)
    for k in range(2):
        found = jnp.where(lane == k, as_col(total_row[:, 128 * k : 128 * k + 128]), found)
    for k in range(4):
        mask = mask_of(k)
        slot_logp = jnp.sum(
            jnp.where(mask, small[k : k + 1] - total_row, 0.0), axis=1, keepdims=True
        )
        used = jnp.max(jnp.where(mask, 1.0, 0.0), axis=1, keepdims=True)
        found = jnp.where(lane == 2 + k, as_col(lse[2 + k : 3 + k]) - slot_logp, found)
        found = jnp.where(lane == 6 + k, used, found)
    off_o[...] = found

    for copy in pending:
        copy.wait_send()

    @pl.loop(0, TILES)
    def _(j):
        v_to, copy = t_send(j)

        @pl.when(v_to != v)
        def _():
            copy.wait_send()

    @pl.when(owner)
    def _():
        for k in range(NY):
            group_send(k).wait_send()
        for copy in z_sends:
            copy.wait_send()

    for i in range(5):
        for side in range(2):

            @pl.when(5 * y + i < TILES)
            def _():
                y_send(5 * y + i, i, side).wait_send()

            j = 5 * (y_down, y_up)[side] + i

            @pl.when(j < TILES)
            def _():
                o_send(j, i, side).wait_send()

    @pl.loop(1, NV)
    def _(k):
        x_send(k).wait_send()


def finish(head_i, s1_i, s2_i, s3_i, s4_i, off_i, head_o, s1_o, s2_o, s3_o, s4_o):
    for k in range(2):
        part = slice(128 * k, 128 * k + 128)
        head_o[part] = head_i[part] - off_i[:, k : k + 1]
    for k, (src, dst) in enumerate(((s1_i, s1_o), (s2_i, s2_o), (s3_i, s3_o), (s4_i, s4_o))):
        used = off_i[:, 6 + k : 7 + k] > 0.5
        dst[...] = jnp.where(used, src[...] - off_i[:, 2 + k : 3 + k], 0.0)


def shards(tokens, cluster_ids, head_weight, cluster_weight, tail_proj, o1, o2, o3, o4):
    widths = [(256, 512), (128, 512), (128, 1024), (128, 1024), (128, 1024)]
    shapes = [jax.ShapeDtypeStruct(s, F32) for s in widths]
    dma = pltpu.SemaphoreType.DMA
    hbm = pl.BlockSpec(memory_space=pltpu.HBM)
    vmem = pl.BlockSpec(memory_space=pltpu.VMEM)
    raw = pl.pallas_call(
        work,
        out_shape=shapes + [jax.ShapeDtypeStruct((128, 128), F32)],
        in_specs=[hbm] * 9,
        out_specs=[vmem] * 6,
        scratch_shapes=[
            pltpu.VMEM((8, 256, 640), BF16),
            pltpu.VMEM((1, 256), jnp.int32),
            pltpu.VMEM((NB, 4, 640, 128), BF16),
            pltpu.VMEM((4, 5120), BF16),
            pltpu.VMEM((160, 2400), BF16),
            pltpu.VMEM((TILES, 2, 80, 128), BF16),
            pltpu.VMEM((NV, 2, 80, 128), BF16),
            pltpu.VMEM((TILES, 128, 128), BF16),
            pltpu.VMEM((1280, 512), BF16),
            pltpu.VMEM((640, 1024), BF16),
            pltpu.VMEM((320, 1024), BF16),
            pltpu.VMEM((160, 1024), BF16),
            pltpu.VMEM((8, 128), F32),
            pltpu.VMEM((NV, 8, 128), F32),
            pltpu.VMEM((4, 128, 256), BF16),
            pltpu.VMEM((8, 256), F32),
            dma((4,)),
            dma((8,)),
            dma((7,)),
            dma((28,)),
            dma((NB, 4)),
            dma((TILES,)),
            dma((NV,)),
            dma((NY,)),
            dma((NY,)),
            dma((NZ,)),
            dma((TILES,)),
            dma((5, 2)),
            dma((TILES,)),
            dma((5, 2)),
            dma((TILES, 2)),
            dma((NV,)),
            dma((NV,)),
        ],
        compiler_params=pltpu.CompilerParams(
            collective_id=0, has_side_effects=True, vmem_limit_bytes=48 * 1024 * 1024
        ),
        name="work",
    )(
        tokens,
        cluster_ids.reshape(1, 256),
        head_weight,
        cluster_weight.T,
        tail_proj,
        o1,
        o2,
        o3,
        o4,
    )
    return tuple(
        pl.pallas_call(
            finish,
            out_shape=shapes,
            in_specs=[vmem] * 6,
            out_specs=[vmem] * 5,
            compiler_params=pltpu.CompilerParams(vmem_limit_bytes=16 * 1024 * 1024),
            name="finish",
        )(*raw)
    )


def solution(mesh):
    in_specs = (
        P("batch", None),
        P("batch", None),
        P("batch", "vocab"),
        P(),
        P("vocab", None),
        P(None, "vocab"),
        P(None, "vocab"),
        P(None, "vocab"),
        P(None, "vocab"),
    )
    return jax.shard_map(
        shards, mesh=mesh, in_specs=in_specs, out_specs=(P("batch", "vocab"),) * 5, check_vma=False
    )
```

time: 162 us -> 65.1 us (0.40)
  the two profiles are of different devices: /device:TPU:6 before, /device:TPU:1 now
where the time goes in v1:
time: 65.1 us; the launch traced here: 64.7 us
  Pallas kernels  57 us (88%)
  local copies, waits for them, and re-layouts  7.04 us (11%)
  between operations  0.66 us (1%)
    pallas_call x1, Pallas kernels, shards(): pl.pallas_call(work, out_shape=shapes + [jax.ShapeDtypeStruct((128, 128),...  55.5 us
    unnamed x14, local copies, waits for them, and re-layouts  7.04 us
    pallas_call x1, Pallas kernels, shards(): pl.pallas_call(finish, out_shape=shapes, in_specs=[vmem] * 6, out_specs=[...  1.57 us

profile of v1, /device:TPU:1, one launch (start us, length us, event | category | flops | bytes accessed | tf_op | source)
XLA Modules:
  0.0 64.7 jit_solution(14215681830684993099)
XLA Ops:
  0.6 0.0 copy-start
  0.6 1.3 %copy-done = bf16[1280,512]{1,0:T(8,128)(2,1)S(1)} copy-done((bf16[1280,512]{1,0:T(8,128)(2,1)S(1)}, bf16[1280,512]{1,0:T(8,128)(2,1)}, u32[]{:S(2)}) %copy-start) | copy-done | bytes 1310744
  2.0 0.0 copy-start.1
  2.0 1.1 %copy-done.1 = bf16[160,2400]{1,0:T(8,128)(2,1)S(1)} copy-done((bf16[160,2400]{1,0:T(8,128)(2,1)S(1)}, bf16[160,2400]{1,0:T(8,128)(2,1)}, u32[]{:S(2)}) %copy-start.1) | copy-done | bytes 768024
  3.1 0.0 copy-start.2
  3.1 1.1 %copy-done.2 = bf16[640,512]{1,0:T(8,128)(2,1)S(1)} copy-done((bf16[640,512]{1,0:T(8,128)(2,1)S(1)}, bf16[640,512]{1,0:T(8,128)(2,1)}, u32[]{:S(2)}) %copy-start.2) | copy-done | bytes 655384
  4.2 0.0 copy-start.3
  4.2 1.1 %copy-done.3 = bf16[320,1024]{1,0:T(8,128)(2,1)S(1)} copy-done((bf16[320,1024]{1,0:T(8,128)(2,1)S(1)}, bf16[320,1024]{1,0:T(8,128)(2,1)}, u32[]{:S(2)}) %copy-start.3) | copy-done | bytes 655384
  5.3 0.0 copy-start.4
  5.3 1.0 %copy-done.4 = bf16[160,1024]{1,0:T(8,128)(2,1)S(1)} copy-done((bf16[160,1024]{1,0:T(8,128)(2,1)S(1)}, bf16[160,1024]{1,0:T(8,128)(2,1)}, u32[]{:S(2)}) %copy-start.4) | copy-done | bytes 327704
  6.2 0.0 copy-start.5
  6.2 0.8 %copy-done.5 = bf16[5120,4]{0,1:T(4,128)(2,1)S(1)} copy-done((bf16[5120,4]{0,1:T(4,128)(2,1)S(1)}, bf16[5120,4]{0,1:T(4,128)(2,1)}, u32[]{:S(2)}) %copy-start.5) | copy-done | bytes 40984
  7.0 0.0 copy-start.6
  7.0 0.7 %copy-done.6 = s32[256,1]{0,1:T(1,128)S(1)} copy-done((s32[256,1]{0,1:T(1,128)S(1)}, s32[256,1]{0,1:T(1,128)}, u32[]{:S(2)}) %copy-start.6) | copy-done | bytes 1048
  7.7 55.5 %work.1 = (f32[256,512]{1,0:T(8,128)S(1)}, f32[128,512]{1,0:T(8,128)S(1)}, f32[128,1024]{1,0:T(8,128)S(1)}, f32[128,1024]{1,0:T(8,128)S(1)}, f32[128,1024]{1,0:T(8,128)S(1)}, /*index=5*/f32[128,128]{1,0:T(8,128)S(1)}) custom-call(bf16[256,5120]{1,0:T(8,128)(2,1)} %tok_h.1, s32[1,256]{1,0:T(1,128)S(1)} %bitcast.3, bf16[640,512]{1,0:T(8,128)(2,1)S(1)} %copy-done.2, ...), custom_call_target="tpu_custom_call" | custom-call | tf_op jit(solution)/shard_map/work/pallas_call | solution.py:446
  63.2 1.6 %finish.1 = (f32[256,512]{1,0:T(8,128)}, f32[128,512]{1,0:T(8,128)}, f32[128,1024]{1,0:T(8,128)}, f32[128,1024]{1,0:T(8,128)}, f32[128,1024]{1,0:T(8,128)}) custom-call(f32[256,512]{1,0:T(8,128)S(1)} %get-tuple-element.11.head_i, f32[128,512]{1,0:T(8,128)S(1)} %get-tuple-element.12.s1_i, f32[128,1024]{1,0:T(8,128)S(1)} %get-tuple-element.13.s2_i, ...), custom_call_target="tpu_custom_call" | custom-call | tf_op jit(solution)/shard_map/finish/pallas_call | solution.py:502
Async XLA Ops:
  0.6 1.3 %copy-start = (bf16[1280,512]{1,0:T(8,128)(2,1)S(1)}, bf16[1280,512]{1,0:T(8,128)(2,1)}, u32[]{:S(2)}) copy-start(bf16[1280,512]{1,0:T(8,128)(2,1)} %o1_h.1) | copy-start | bytes 3932164
  2.0 1.1 %copy-start.1 = (bf16[160,2400]{1,0:T(8,128)(2,1)S(1)}, bf16[160,2400]{1,0:T(8,128)(2,1)}, u32[]{:S(2)}) copy-start(bf16[160,2400]{1,0:T(8,128)(2,1)} %t_h.1) | copy-start | bytes 2304004
  3.1 1.1 %copy-start.2 = (bf16[640,512]{1,0:T(8,128)(2,1)S(1)}, bf16[640,512]{1,0:T(8,128)(2,1)}, u32[]{:S(2)}) copy-start(bf16[640,512]{1,0:T(8,128)(2,1)} %w_h.1) | copy-start | bytes 1966084
  4.2 1.1 %copy-start.3 = (bf16[320,1024]{1,0:T(8,128)(2,1)S(1)}, bf16[320,1024]{1,0:T(8,128)(2,1)}, u32[]{:S(2)}) copy-start(bf16[320,1024]{1,0:T(8,128)(2,1)} %o3_h.1) | copy-start | bytes 1966084
  5.3 1.0 %copy-start.4 = (bf16[160,1024]{1,0:T(8,128)(2,1)S(1)}, bf16[160,1024]{1,0:T(8,128)(2,1)}, u32[]{:S(2)}) copy-start(bf16[160,1024]{1,0:T(8,128)(2,1)} %o4_h.1) | copy-start | bytes 983044
  6.2 0.8 %copy-start.5 = (bf16[5120,4]{0,1:T(4,128)(2,1)S(1)}, bf16[5120,4]{0,1:T(4,128)(2,1)}, u32[]{:S(2)}) copy-start(bf16[5120,4]{0,1:T(4,128)(2,1)} %param.12) | copy-start | bytes 122884
  7.0 0.7 %copy-start.6 = (s32[256,1]{0,1:T(1,128)S(1)}, s32[256,1]{0,1:T(1,128)}, u32[]{:S(2)}) copy-start(s32[256,1]{0,1:T(1,128)} %param.10) | copy-start | bytes 3076

commit v2 on v1

--- a/solution.py
+++ b/solution.py
@@ -54,6 +54,16 @@
 
     load_t = pltpu.make_async_copy(t_h, tin, ld_misc.at[0])
     load_t.start()
+    barrier = pltpu.get_barrier_semaphore()
+    for peer in (right, left, mate):
+        pl.semaphore_signal(barrier, inc=1, device_id=(v, peer), device_id_type=pl.DeviceIdType.MESH)
+
+    @pl.loop(1, NV)
+    def _(k):
+        pl.semaphore_signal(
+            barrier, inc=1, device_id=(lax.rem(v + k, NV), b), device_id_type=pl.DeviceIdType.MESH
+        )
+
     load_w = [
         pltpu.make_async_copy(w_h.at[:, pl.ds(128 * q, 128)], wbuf.at[b, q], ld_w.at[q])
         for q in range(4)
@@ -77,16 +87,6 @@
     for copy in load_out:
         copy.start()
 
-    barrier = pltpu.get_barrier_semaphore()
-    for peer in (right, left, mate):
-        pl.semaphore_signal(barrier, inc=1, device_id=(v, peer), device_id_type=pl.DeviceIdType.MESH)
-
-    @pl.loop(1, NV)
-    def _(k):
-        pl.semaphore_signal(
-            barrier, inc=1, device_id=(lax.rem(v + k, NV), b), device_id_type=pl.DeviceIdType.MESH
-        )
-
     load_t.wait()
     for j in range(TILES - 1):
         for h in range(2):
@@ -95,10 +95,24 @@
         tv[TILES - 1, h] = jnp.concatenate(
             [tin[80 * h : 80 * h + 80, 2304:2400], jnp.zeros((80, 32), BF16)], axis=1
         )
+    pl.semaphore_wait(barrier, 3 + NV - 1)
+
+    def t_send(j):
+        y_to = j // 5
+        v_to = y_to * NZ + ring_place(lax.rem(j, 5), y_to)
+        sends = jnp.logical_and(v_to != v, lax.rem(j, 2) == c)
+        return sends, remote(tv.at[j], town.at[v], tss.at[j], trs.at[v], v_to, b)
+
+    @pl.loop(0, TILES)
+    def _(k):
+        sends, copy = t_send(lax.rem(k + v, TILES))
+
+        @pl.when(sends)
+        def _():
+            copy.start()
+
     for copy in load_w:
         copy.wait()
-    pl.semaphore_wait(barrier, 3 + NV - 1)
-
     def w_send(shard, q, to, k):
         return remote(wbuf.at[shard, q], wbuf.at[shard, q], wss.at[k], wrs.at[shard, q], v, to)
 
@@ -113,19 +127,6 @@
         start(w_send(b, (k + 2) % 4, left, 4 + k))
     for k in range(4):
         start(w_send(b, k, mate, 8 + k))
-
-    def t_send(j):
-        y_to = j // 5
-        v_to = y_to * NZ + ring_place(lax.rem(j, 5), y_to)
-        return v_to, remote(tv.at[j, c], town.at[v, c], tss.at[j], trs.at[v], v_to, b)
-
-    @pl.loop(0, TILES)
-    def _(jj):
-        v_to, copy = t_send(lax.rem(jj + v, TILES))
-
-        @pl.when(v_to != v)
-        def _():
-            copy.start()
 
     mine_r = lax.rem(z - 2 * y + 8, NZ)
     mine_i = (5 * mine_r + 7) // 8
@@ -165,39 +166,41 @@
     for copy in load_out:
         copy.wait()
 
-    def head_add(shard, q):
-        cols = slice(128 * q, 128 * q + 128)
-        head_o[:, cols] += jnp.dot(tok[shard], wbuf[shard, q], preferred_element_type=F32)
-
-    for q in range(4):
-        head_o[:, 128 * q : 128 * q + 128] = jnp.dot(
-            tok[b], wbuf[b, q], preferred_element_type=F32
-        )
+    def product(shard, h):
+        pair = jnp.concatenate([wbuf[shard, 2 * h], wbuf[shard, 2 * h + 1]], axis=1)
+        return jnp.dot(tok[shard], pair, preferred_element_type=F32)
+
+    def head_add(shard, h):
+        head_o[:, 256 * h : 256 * h + 256] += product(shard, h)
+
+    for h in range(2):
+        head_o[:, 256 * h : 256 * h + 256] = product(b, h)
 
     from_left = [(left, 0), (left, 1), (left, 2), (left, 3), (far, 0), (far, 1)]
     from_right = [(right, 2), (right, 3), (right, 0), (right, 1), (far, 2), (far, 3)]
     flip = 1 - 2 * c
 
-    def w_step(s):
+    def w_take(s):
         for side, (shard, q) in enumerate((from_left[s], from_right[s])):
             arrived(wbuf.at[shard, q], wrs.at[shard, q])
             if s < 2:
                 start(w_send(shard, q, (right, left)[side], 12 + 2 * s + side))
             start(w_send(shard, q, mate, 16 + 2 * s + side))
-        for shard, q in (from_left[s], from_right[s]):
-            head_add(shard, q)
-
-    def w_mate(s):
-        for shard, q in (from_left[s], from_right[s]):
-            arrived(wbuf.at[shard + flip, q], wrs.at[shard + flip, q])
-            head_add(shard + flip, q)
-
-    for q in range(4):
-        arrived(wbuf.at[mate, q], wrs.at[mate, q])
-        head_add(mate, q)
-    w_step(0)
-    w_step(1)
-    w_mate(0)
+
+    def w_use(p):
+        pairs = (from_left[2 * p : 2 * p + 2], from_right[2 * p : 2 * p + 2])
+        for pair in pairs:
+            head_add(pair[0][0], pair[0][1] // 2)
+        for pair in pairs:
+            for shard, q in pair:
+                arrived(wbuf.at[shard + flip, q], wrs.at[shard + flip, q])
+            head_add(pair[0][0] + flip, pair[0][1] // 2)
+
+    for h in range(2):
+        for q in (2 * h, 2 * h + 1):
+            arrived(wbuf.at[mate, q], wrs.at[mate, q])
+        head_add(mate, h)
+    w_take(0)
 
     z_sends = [
         remote(
@@ -208,32 +211,40 @@
             y * NZ + lax.rem(z + k, NZ),
             b,
         )
-        for k in range(1, NZ)
+        for k in (4, 3, 5, 2, 6, 1, 7)
     ]
 
     def group_send(k):
-        g = lax.rem(y + k, NY)
-        part = town.at[pl.ds(8 * g, 8), c]
-        return remote(part, part, tpss.at[g], tprs.at[g], v, mate)
+        part = town.at[pl.ds(8 * lax.rem(y + k, NY), 8)]
+        return remote(part, part, tpss.at[k], tprs.at[k], v, mate)
+
+    first = jnp.logical_and(owner, lax.rem(mine_j, 2) == c)
+    second = jnp.logical_and(owner, lax.rem(mine_j, 2) != c)
+
+    @pl.when(first)
+    def _():
+        town[v] = tv[mine_j]
 
     @pl.when(owner)
     def _():
-        town[v, c] = tv[mine_j, c]
-        for k in range(NY):
-            g = lax.rem(y + k, NY)
-
-            @pl.loop(0, NZ)
-            def _(s):
-                @pl.when(8 * g + s != v)
-                def _():
-                    arrived(town.at[8 * g + s, c], trs.at[8 * g + s])
-
-            group_send(k).start()
         total = jnp.zeros((256, 128), F32)
         for k in range(NY):
             g = lax.rem(y + k, NY)
-            part = town.at[pl.ds(8 * g, 8), 1 - c]
-            arrived(part, tprs.at[g])
+
+            @pl.when(first)
+            def _():
+                @pl.loop(0, NZ)
+                def _(s):
+                    @pl.when(8 * g + s != v)
+                    def _():
+                        arrived(town.at[8 * g + s], trs.at[8 * g + s])
+
+                group_send(k).start()
+
+            @pl.when(second)
+            def _():
+                arrived(town.at[pl.ds(8 * g, 8)], tprs.at[k])
+
             for h in range(2):
                 total += jnp.dot(
                     tok[2 * g + h],
@@ -260,8 +271,8 @@
         for copy in z_sends:
             copy.start()
 
-    w_step(2)
-    w_mate(1)
+    w_take(1)
+    w_take(2)
 
     def y_send(j, i, side):
         return remote(
@@ -277,25 +288,19 @@
         part = pbuf.at[j, pl.ds(64 * side, 64)]
         return remote(part, part, poss.at[i, side], pors.at[j, side], (y_up, y_down)[side] * NZ + z, b)
 
-    for k in range(5):
-        i = lax.rem(mine_i + k, 5)
+    def relay_z(i):
         j = 5 * y + i
+
+        @pl.when(jnp.logical_and(j < TILES, jnp.logical_not(jnp.logical_and(owner, mine_i == i))))
+        def _():
+            arrived(pbuf.at[j], pzrs.at[j])
 
         @pl.when(j < TILES)
         def _():
-            if k == 0:
-
-                @pl.when(jnp.logical_not(owner))
-                def _():
-                    arrived(pbuf.at[j], pzrs.at[j])
-            else:
-                arrived(pbuf.at[j], pzrs.at[j])
             for side in range(2):
                 y_send(j, i, side).start()
 
-    w_step(3)
-    w_mate(2)
-    for i in range(5):
+    def relay_y(i):
         for side, ring in enumerate((y_down, y_up)):
             j = 5 * ring + i
 
@@ -304,8 +309,57 @@
                 arrived(pbuf.at[j], pyrs.at[j])
                 o_send(j, i, side).start()
 
-    w_step(4)
-    w_mate(3)
+    for i in range(5):
+        relay_z(i)
+        if i == 2:
+            w_use(0)
+            w_take(3)
+    w_use(1)
+    for i in range(5):
+        relay_y(i)
+        if i == 2:
+            w_take(4)
+    w_take(5)
+    eye = lax.broadcasted_iota(jnp.int32, (128, 128), 0) == lax.broadcasted_iota(
+        jnp.int32, (128, 128), 1
+    )
+
+    def as_row(col):
+        return jnp.sum(jnp.where(eye, col, 0.0), axis=0, keepdims=True)
+
+    def as_col(row):
+        return jnp.sum(jnp.where(eye, row, 0.0), axis=1, keepdims=True)
+
+    def tiles(lo, hi):
+        return jnp.concatenate([pbuf[t] for t in range(lo, hi)], axis=1)
+
+    def score(ring):
+        if ring < 2:
+            s1_o[...] += jnp.dot(
+                tiles(5 * ring, 5 * ring + 5),
+                o1[640 * ring : 640 * ring + 640],
+                preferred_element_type=F32,
+            )
+        elif ring == 2:
+            s2_o[...] = jnp.dot(tiles(10, 15), o2[...], preferred_element_type=F32)
+        else:
+            split = pbuf[17]
+            s3_o[...] = jnp.dot(
+                jnp.concatenate([tiles(15, 17), split[:, :64]], axis=1),
+                o3[...],
+                preferred_element_type=F32,
+            )
+            s4_o[...] = jnp.dot(
+                jnp.concatenate([split[:, 64:], pbuf[18][:, :96]], axis=1),
+                o4[...],
+                preferred_element_type=F32,
+            )
+
+    s1_o[...] = jnp.zeros_like(s1_o)
+    for ring in range(NY):
+        pl.when(y_far != ring)(lambda: score(ring))
+    w_use(2)
+    head_rows = [as_row(log_sum(head_o[128 * k : 128 * k + 128])) for k in range(2)]
     for i in range(5):
         j = 5 * y_far + i
 
@@ -315,40 +369,9 @@
                 part = pbuf.at[j, pl.ds(64 * side, 64)]
                 arrived(part, pors.at[j, side])
 
-    s1_o[...] = jnp.dot(
-        jnp.concatenate([pbuf[t] for t in range(10)], axis=1), o1[...], preferred_element_type=F32
-    )
-    s2_o[...] = jnp.dot(
-        jnp.concatenate([pbuf[t] for t in range(10, 15)], axis=1),
-        o2[...],
-        preferred_element_type=F32,
-    )
-    split = pbuf[17]
-    s3_o[...] = jnp.dot(
-        jnp.concatenate([pbuf[15], pbuf[16], split[:, :64]], axis=1),
-        o3[...],
-        preferred_element_type=F32,
-    )
-    s4_o[...] = jnp.dot(
-        jnp.concatenate([split[:, 64:], pbuf[18][:, :96]], axis=1),
-        o4[...],
-        preferred_element_type=F32,
-    )
-    eye = lax.broadcasted_iota(jnp.int32, (128, 128), 0) == lax.broadcasted_iota(
-        jnp.int32, (128, 128), 1
-    )
-
-    def as_row(col):
-        return jnp.sum(jnp.where(eye, col, 0.0), axis=0, keepdims=True)
-
-    def as_col(row):
-        return jnp.sum(jnp.where(eye, row, 0.0), axis=1, keepdims=True)
-
+    for ring in range(NY):
+        pl.when(y_far == ring)(lambda: score(ring))
     tail_rows = [as_row(log_sum(ref[...])) for ref in (s1_o, s2_o, s3_o, s4_o)]
-    w_step(5)
-    w_mate(4)
-    w_mate(5)
-    head_rows = [as_row(log_sum(head_o[128 * k : 128 * k + 128])) for k in range(2)]
     packed = jnp.concatenate(head_rows + tail_rows + [jnp.zeros((2, 128), F32)], axis=0)
     msg[...] = packed
     xbuf[v] = packed
@@ -364,6 +387,40 @@
     small = rows[0:4]
     small_top = jnp.max(small, axis=0, keepdims=True)
     small_sum = jnp.sum(jnp.exp(small - small_top), axis=0, keepdims=True)
+
+    for copy in pending:
+        copy.wait_send()
+
+    @pl.loop(0, TILES)
+    def _(j):
+        sends, copy = t_send(j)
+
+        @pl.when(sends)
+        def _():
+            copy.wait_send()
+
+    @pl.when(first)
+    def _():
+        for k in range(NY):
+            group_send(k).wait_send()
+
+    @pl.when(owner)
+    def _():
+        for copy in z_sends:
+            copy.wait_send()
+
+    for i in range(5):
+        for side in range(2):
+
+            @pl.when(5 * y + i < TILES)
+            def _():
+                y_send(5 * y + i, i, side).wait_send()
+
+            j = 5 * (y_down, y_up)[side] + i
+
+            @pl.when(j < TILES)
+            def _():
+                o_send(j, i, side).wait_send()
 
     @pl.loop(1, NV)
     def _(k):
@@ -392,60 +449,45 @@
         found = jnp.where(lane == 6 + k, used, found)
     off_o[...] = found
 
-    for copy in pending:
-        copy.wait_send()
-
-    @pl.loop(0, TILES)
-    def _(j):
-        v_to, copy = t_send(j)
-
-        @pl.when(v_to != v)
-        def _():
-            copy.wait_send()
-
-    @pl.when(owner)
-    def _():
-        for k in range(NY):
-            group_send(k).wait_send()
-        for copy in z_sends:
-            copy.wait_send()
-
-    for i in range(5):
-        for side in range(2):
-
-            @pl.when(5 * y + i < TILES)
-            def _():
-                y_send(5 * y + i, i, side).wait_send()
-
-            j = 5 * (y_down, y_up)[side] + i
-
-            @pl.when(j < TILES)
-            def _():
-                o_send(j, i, side).wait_send()
-
     @pl.loop(1, NV)
     def _(k):
         x_send(k).wait_send()
 
 
-def finish(head_i, s1_i, s2_i, s3_i, s4_i, off_i, head_o, s1_o, s2_o, s3_o, s4_o):
+def finish(
+    head_i, s1_i, s2_i, s3_i, s4_i, off_i,
+    head_o, s1_o, s2_o, s3_o, s4_o,
+    head_v, s1_v, s2_v, s3_v, s4_v, sems,
+):
+    copies = []
+
+    def write(src, dst, sem):
+        copies.append(pltpu.make_async_copy(src, dst, sem))
+        copies[-1].start()
+
     for k in range(2):
         part = slice(128 * k, 128 * k + 128)
-        head_o[part] = head_i[part] - off_i[:, k : k + 1]
-    for k, (src, dst) in enumerate(((s1_i, s1_o), (s2_i, s2_o), (s3_i, s3_o), (s4_i, s4_o))):
-        used = off_i[:, 6 + k : 7 + k] > 0.5
-        dst[...] = jnp.where(used, src[...] - off_i[:, 2 + k : 3 + k], 0.0)
+        head_v[part] = head_i[part] - off_i[:, k : k + 1]
+        write(head_v.at[part], head_o.at[part], sems.at[k])
+    tails = ((s2_i, s2_v, s2_o), (s3_i, s3_v, s3_o), (s4_i, s4_v, s4_o), (s1_i, s1_v, s1_o))
+    for at, (src, held, dst) in zip((1, 2, 3, 0), tails):
+        used = off_i[:, 6 + at : 7 + at] > 0.5
+        held[...] = jnp.where(used, src[...] - off_i[:, 2 + at : 3 + at], 0.0)
+        write(held, dst, sems.at[2 + at])
+    for copy in copies:
+        copy.wait()
 
 
 def shards(tokens, cluster_ids, head_weight, cluster_weight, tail_proj, o1, o2, o3, o4):
     widths = [(256, 512), (128, 512), (128, 1024), (128, 1024), (128, 1024)]
     shapes = [jax.ShapeDtypeStruct(s, F32) for s in widths]
+    held = [pltpu.VMEM(s, F32) for s in widths + [(128, 128)]]
     dma = pltpu.SemaphoreType.DMA
     hbm = pl.BlockSpec(memory_space=pltpu.HBM)
     vmem = pl.BlockSpec(memory_space=pltpu.VMEM)
     raw = pl.pallas_call(
         work,
-        out_shape=shapes + [jax.ShapeDtypeStruct((128, 128), F32)],
+        out_shape=held,
         in_specs=[hbm] * 9,
         out_specs=[vmem] * 6,
         scratch_shapes=[
@@ -484,7 +526,7 @@
             dma((NV,)),
         ],
         compiler_params=pltpu.CompilerParams(
-            collective_id=0, has_side_effects=True, vmem_limit_bytes=48 * 1024 * 1024
+            collective_id=0, has_side_effects=True, vmem_limit_bytes=67043328 - 2560 * 1024
         ),
         name="work",
     )(
@@ -503,7 +545,8 @@
             finish,
             out_shape=shapes,
             in_specs=[vmem] * 6,
-            out_specs=[vmem] * 5,
+            out_specs=[hbm] * 5,
+            scratch_shapes=[pltpu.VMEM(s, F32) for s in widths] + [dma((6,))],
             compiler_params=pltpu.CompilerParams(vmem_limit_bytes=16 * 1024 * 1024),
             name="finish",
         )(*raw)

time: 65.1 us -> 51.2 us (0.79)
  the two profiles are of different devices: /device:TPU:1 before, /device:TPU:6 now
where the time goes in v2:
time: 51.2 us; the launch traced here: 51.1 us
  Pallas kernels  50.5 us (99%)
  between operations  0.64 us (1%)
    pallas_call x1, Pallas kernels, shards(): pl.pallas_call(work, out_shape=held, in_specs=[hbm] * 9, out_specs=[vmem]...  48.9 us
    pallas_call x1, Pallas kernels, shards(): pl.pallas_call(finish, out_shape=shapes, in_specs=[vmem] * 6, out_specs=[...  1.53 us

profile of v2, /device:TPU:6, one launch (start us, length us, event | category | flops | bytes accessed | tf_op | source)
XLA Modules:
  0.0 51.1 jit_solution(1472773980604855253)
XLA Ops:
  0.6 48.9 %work.1 = (f32[256,512]{1,0:T(8,128)S(1)}, f32[128,512]{1,0:T(8,128)S(1)}, f32[128,1024]{1,0:T(8,128)S(1)}, f32[128,1024]{1,0:T(8,128)S(1)}, f32[128,1024]{1,0:T(8,128)S(1)}, /*index=5*/f32[128,128]{1,0:T(8,128)S(1)}) custom-call(bf16[256,5120]{1,0:T(8,128)(2,1)} %tok_h.1, s32[1,256]{1,0:T(1,128)} %bitcast.3, bf16[640,512]{1,0:T(8,128)(2,1)} %w_h.1, ...), custom_call_target="tpu_custom_call" | custom-call | tf_op jit(solution)/shard_map/work/pallas_call | solution.py:488
  49.6 1.5 %finish.1 = (f32[256,512]{1,0:T(8,128)}, f32[128,512]{1,0:T(8,128)}, f32[128,1024]{1,0:T(8,128)}, f32[128,1024]{1,0:T(8,128)}, f32[128,1024]{1,0:T(8,128)}) custom-call(f32[256,512]{1,0:T(8,128)S(1)} %get-tuple-element.11.head_i, f32[128,512]{1,0:T(8,128)S(1)} %get-tuple-element.12.s1_i, f32[128,1024]{1,0:T(8,128)S(1)} %get-tuple-element.13.s2_i, ...), custom_call_target="tpu_custom_call" | custom-call | tf_op jit(solution)/shard_map/finish/pallas_call | solution.py:544

commit v3 on v2

--- a/solution.py
+++ b/solution.py
@@ -39,7 +39,7 @@
 def work(
     tok_h, ids_h, w_h, cw_h, t_h, o1_h, o2_h, o3_h, o4_h,
     head_o, s1_o, s2_o, s3_o, s4_o, off_o,
-    tok, ids, wbuf, cw, tin, tv, town, pbuf, o1, o2, o3, o4, msg, xbuf, pick, rows,
+    tok, ids, wbuf, cw, tin, tv, town, pbuf, o1, o2, o3, o4, msg, xbuf, pick, wide, known, rows,
     ld_w, ld_tok, ld_misc,
     wss, wrs, tss, trs, tpss, tprs, pzss, pzrs, pyss, pyrs, poss, pors, xss, xrs,
 ):
@@ -150,7 +150,9 @@
         return jnp.logical_and(id_row == k, slot_row == slots)
 
     for k in range(4):
-        pick[k] = jnp.where(mask_of(k), 1.0, 0.0).astype(BF16)
+        chosen = jnp.where(mask_of(k), 1.0, 0.0)
+        wide[k] = chosen
+        pick[k] = chosen.astype(BF16)
     for copy in load_tok:
         copy.wait()
     load_cw.wait()
@@ -162,7 +164,17 @@
             (((1,), (1,)), ((), ())),
             preferred_element_type=F32,
         )
-    rows[0:4] = small
+    small_top = jnp.max(small, axis=0, keepdims=True)
+    rows[0:1] = small_top
+    rows[1:2] = jnp.sum(jnp.exp(small - small_top), axis=0, keepdims=True)
+    lane = lax.broadcasted_iota(jnp.int32, (128, 128), 1)
+    before_lse = jnp.zeros((128, 128), F32)
+    for k in range(4):
+        logit = jnp.sum(wide[k] * small[k : k + 1], axis=1, keepdims=True)
+        used = jnp.sum(wide[k], axis=1, keepdims=True)
+        before_lse = jnp.where(lane == 2 + k, -logit, before_lse)
+        before_lse = jnp.where(lane == 6 + k, used, before_lse)
+    known[...] = before_lse
     for copy in load_out:
         copy.wait()
 
@@ -384,10 +396,6 @@
     def _(k):
         x_send(k).start()
 
-    small = rows[0:4]
-    small_top = jnp.max(small, axis=0, keepdims=True)
-    small_sum = jnp.sum(jnp.exp(small - small_top), axis=0, keepdims=True)
-
     for copy in pending:
         copy.wait_send()
 
@@ -431,22 +439,20 @@
     top = jnp.max(every, axis=0)
     lse = top + jnp.log(jnp.sum(jnp.exp(every - top[None]), axis=0))
     head_lse = jnp.concatenate([lse[0:1], lse[1:2]], axis=1)
+    small_top, small_sum = rows[0:1], rows[1:2]
     overall = jnp.maximum(head_lse, small_top)
     total_row = overall + jnp.log(
         jnp.exp(head_lse - overall) + small_sum * jnp.exp(small_top - overall)
     )
-    lane = lax.broadcasted_iota(jnp.int32, (128, 128), 1)
-    found = jnp.zeros((128, 128), F32)
+    found = known[...]
     for k in range(2):
         found = jnp.where(lane == k, as_col(total_row[:, 128 * k : 128 * k + 128]), found)
     for k in range(4):
-        mask = mask_of(k)
-        slot_logp = jnp.sum(
-            jnp.where(mask, small[k : k + 1] - total_row, 0.0), axis=1, keepdims=True
-        )
-        used = jnp.max(jnp.where(mask, 1.0, 0.0), axis=1, keepdims=True)
-        found = jnp.where(lane == 2 + k, as_col(lse[2 + k : 3 + k]) - slot_logp, found)
-        found = jnp.where(lane == 6 + k, used, found)
+        both = jnp.where(eye, lse[2 + k : 3 + k], 0.0)
+        for h in range(2):
+            part = slice(128 * h, 128 * h + 128)
+            both += wide[k, :, part] * total_row[:, part]
+        found += jnp.where(lane == 2 + k, jnp.sum(both, axis=1, keepdims=True), 0.0)
     off_o[...] = found
 
     @pl.loop(1, NV)
@@ -506,6 +512,8 @@
             pltpu.VMEM((8, 128), F32),
             pltpu.VMEM((NV, 8, 128), F32),
             pltpu.VMEM((4, 128, 256), BF16),
+            pltpu.VMEM((4, 128, 256), F32),
+            pltpu.VMEM((128, 128), F32),
             pltpu.VMEM((8, 256), F32),
             dma((4,)),
             dma((8,)),

time: 51.2 us -> 51.1 us (level)
  no operation moved by 1% of the time
where the time goes in v3:
time: 51.1 us; the launch traced here: 51 us
  Pallas kernels  50.4 us (99%)
  between operations  0.64 us (1%)
    pallas_call x1, Pallas kernels, shards(): pl.pallas_call(work, out_shape=held, in_specs=[hbm] * 9, out_specs=[vmem]...  48.8 us
    pallas_call x1, Pallas kernels, shards(): pl.pallas_call(finish, out_shape=shapes, in_specs=[vmem] * 6, out_specs=[...  1.53 us

profile of v3, /device:TPU:6, one launch (start us, length us, event | category | flops | bytes accessed | tf_op | source)
XLA Modules:
  0.0 51.0 jit_solution(4676117388858352116)
XLA Ops:
  0.6 48.8 %work.1 = (f32[256,512]{1,0:T(8,128)S(1)}, f32[128,512]{1,0:T(8,128)S(1)}, f32[128,1024]{1,0:T(8,128)S(1)}, f32[128,1024]{1,0:T(8,128)S(1)}, f32[128,1024]{1,0:T(8,128)S(1)}, /*index=5*/f32[128,128]{1,0:T(8,128)S(1)}) custom-call(bf16[256,5120]{1,0:T(8,128)(2,1)} %tok_h.1, s32[1,256]{1,0:T(1,128)} %bitcast.3, bf16[640,512]{1,0:T(8,128)(2,1)} %w_h.1, ...), custom_call_target="tpu_custom_call" | custom-call | tf_op jit(solution)/shard_map/work/pallas_call | solution.py:494
  49.5 1.5 %finish.1 = (f32[256,512]{1,0:T(8,128)}, f32[128,512]{1,0:T(8,128)}, f32[128,1024]{1,0:T(8,128)}, f32[128,1024]{1,0:T(8,128)}, f32[128,1024]{1,0:T(8,128)}) custom-call(f32[256,512]{1,0:T(8,128)S(1)} %get-tuple-element.11.head_i, f32[128,512]{1,0:T(8,128)S(1)} %get-tuple-element.12.s1_i, f32[128,1024]{1,0:T(8,128)S(1)} %get-tuple-element.13.s2_i, ...), custom_call_target="tpu_custom_call" | custom-call | tf_op jit(solution)/shard_map/finish/pallas_call | solution.py:552

commit v4 on v3

--- a/solution.py
+++ b/solution.py
@@ -321,27 +321,6 @@
                 arrived(pbuf.at[j], pyrs.at[j])
                 o_send(j, i, side).start()
 
-    for i in range(5):
-        relay_z(i)
-        if i == 2:
-            w_use(0)
-            w_take(3)
-    w_use(1)
-    for i in range(5):
-        relay_y(i)
-        if i == 2:
-            w_take(4)
-    w_take(5)
-    eye = lax.broadcasted_iota(jnp.int32, (128, 128), 0) == lax.broadcasted_iota(
-        jnp.int32, (128, 128), 1
-    )
-
-    def as_row(col):
-        return jnp.sum(jnp.where(eye, col, 0.0), axis=0, keepdims=True)
-
-    def as_col(row):
-        return jnp.sum(jnp.where(eye, row, 0.0), axis=1, keepdims=True)
-
     def tiles(lo, hi):
         return jnp.concatenate([pbuf[t] for t in range(lo, hi)], axis=1)
 
@@ -368,8 +347,32 @@
             )
 
     s1_o[...] = jnp.zeros_like(s1_o)
+    for i in range(5):
+        relay_z(i)
+        if i == 2:
+            w_use(0)
+            w_take(3)
+    w_use(1)
     for ring in range(NY):
-        pl.when(y_far != ring)(lambda: score(ring))
+        pl.when(y == ring)(lambda: score(ring))
+    for i in range(5):
+        relay_y(i)
+        if i == 1:
+            w_take(4)
+        if i == 3:
+            w_take(5)
+    eye = lax.broadcasted_iota(jnp.int32, (128, 128), 0) == lax.broadcasted_iota(
+        jnp.int32, (128, 128), 1
+    )
+
+    def as_row(col):
+        return jnp.sum(jnp.where(eye, col, 0.0), axis=0, keepdims=True)
+
+    def as_col(row):
+        return jnp.sum(jnp.where(eye, row, 0.0), axis=1, keepdims=True)
+
+    for ring in range(NY):
+        pl.when(jnp.logical_or(y_up == ring, y_down == ring))(lambda: score(ring))
     w_use(2)
     head_rows = [as_row(log_sum(head_o[128 * k : 128 * k + 128])) for k in range(2)]
     for i in range(5):

time: 51.1 us -> 51.1 us (level)
  no operation moved by 1% of the time
where the time goes in v4:
time: 51.1 us; the launch traced here: 51 us
  Pallas kernels  50.4 us (99%)
  between operations  0.64 us (1%)
    pallas_call x1, Pallas kernels, shards(): pl.pallas_call(work, out_shape=held, in_specs=[hbm] * 9, out_specs=[vmem]...  48.9 us
    pallas_call x1, Pallas kernels, shards(): pl.pallas_call(finish, out_shape=shapes, in_specs=[vmem] * 6, out_specs=[...  1.53 us

profile of v4, /device:TPU:6, one launch (start us, length us, event | category | flops | bytes accessed | tf_op | source)
XLA Modules:
  0.0 51.0 jit_solution(10969402248559052325)
XLA Ops:
  0.6 48.9 %work.1 = (f32[256,512]{1,0:T(8,128)S(1)}, f32[128,512]{1,0:T(8,128)S(1)}, f32[128,1024]{1,0:T(8,128)S(1)}, f32[128,1024]{1,0:T(8,128)S(1)}, f32[128,1024]{1,0:T(8,128)S(1)}, /*index=5*/f32[128,128]{1,0:T(8,128)S(1)}) custom-call(bf16[256,5120]{1,0:T(8,128)(2,1)} %tok_h.1, s32[1,256]{1,0:T(1,128)} %bitcast.3, bf16[640,512]{1,0:T(8,128)(2,1)} %w_h.1, ...), custom_call_target="tpu_custom_call" | custom-call | tf_op jit(solution)/shard_map/work/pallas_call | solution.py:497
  49.5 1.5 %finish.1 = (f32[256,512]{1,0:T(8,128)}, f32[128,512]{1,0:T(8,128)}, f32[128,1024]{1,0:T(8,128)}, f32[128,1024]{1,0:T(8,128)}, f32[128,1024]{1,0:T(8,128)}) custom-call(f32[256,512]{1,0:T(8,128)S(1)} %get-tuple-element.11.head_i, f32[128,512]{1,0:T(8,128)S(1)} %get-tuple-element.12.s1_i, f32[128,1024]{1,0:T(8,128)S(1)} %get-tuple-element.13.s2_i, ...), custom_call_target="tpu_custom_call" | custom-call | tf_op jit(solution)/shard_map/finish/pallas_call | solution.py:555
